TPU v7x, 32 devices: a whole 2x2x4 slice. The times are simulated.
32 devices in a mesh: group: 2 (over y), tm: 4 (over z), space: 2 (over x), head: 2 (over core).
Axes of the slice: x: 2, y: 2, z: 4, core: 2. Of those that a mesh axis runs over, the one named last changes fastest.
Arguments:
- queries: bfloat16 [8, 16, 32, 3072], P(('group', 'tm'), 'space', None, 'head'), parts along dimension 0, may hold values from -5.5 to 5.5
- keys: bfloat16 [8, 16, 32, 3072], P(('group', 'tm'), 'space', None, 'head'), parts along dimension 0, may hold values from -5.5 to 5.5
- values: bfloat16 [8, 16, 32, 3072], P(('group', 'tm'), 'space', None, 'head'), parts along dimension 0, may hold values from -6 to 6
- window: int32 [8, 2, 4, 27], P(('group', 'tm'), 'space'), parts along dimension 0, may hold values 0 or 1
Outputs:
- attended: bfloat16 [8, 16, 32, 3072], P(('group', 'tm'), 'space', None, 'head'), parts along dimension 0
There are 2 independent parts, one for each index of `group`. A program takes and returns all parts, laid end to end along the dimension named above; each array names one. Nothing has to cross between parts.
Inputs may be any that keep to these rules, and one draw needn't show every extreme that they name: `window`: slot dt * 9 + (dy + 1) * 3 + (dx + 1) of a query tile's entry enables the key tile dt frames earlier, dy tile rows and dx tile columns away; slot 4, the tile itself, is attended whatever it holds.
All inputs are finite; a program needn't handle non-finite values. No bound on the sum of `window` on one device may be relied on, other than what follows from the above.
Results may differ from a plain program's by a relative error of at most 0.0046.
Values may be sent and summed in bfloat16 or wider, within the bound.
A program may use at most 128 MiB of HBM per device.

v0:
```python
import functools
import math

import jax
import jax.numpy as jnp
from jax import lax
from jax.experimental import pallas as pl
from jax.experimental.pallas import tpu as pltpu
from jax.sharding import PartitionSpec as P

HDIM = 128
TILE = 8
EXTRA = 8
FAR_LAG, PASS_LAG, LAST_LAG = 1, 3, 5
MASKED = -float(2**17)
EXP2_SCALE = HDIM ** (-0.5) * math.log2(math.e)
MESH = pl.DeviceIdType.MESH


def remote(src, dst, send_sem, recv_sem, device):
    return pltpu.make_async_remote_copy(
        src_ref=src,
        dst_ref=dst,
        send_sem=send_sem,
        recv_sem=recv_sem,
        device_id=device,
        device_id_type=MESH,
    )


def kernel(
    frames,
    rows,
    q_hbm,
    k_hbm,
    v_hbm,
    win_ref,
    out_ref,
    q_all,
    kv_all,
    qb_all,
    kone,
    o_send,
    o_recv,
    o_own,
    lse_own,
    load_sem,
    kv_send_sem,
    kv_recv_sem,
    q_send_sem,
    q_recv_sem,
    o_send_sem,
    o_recv_sem,
):
    frame = lax.axis_index("tm")
    row = lax.axis_index("space")
    heads = q_all.shape[1]
    columns = q_all.shape[3]
    tile_cols = columns // TILE
    tokens = TILE * columns
    has1 = frame + 1 < frames
    has2 = frame + 2 < frames
    prev1 = frame >= 1
    if rows == 1:
        sides = []
    elif rows == 2:
        sides = [(0, 1 - row, None, 1 - 2 * row, 0)]
    else:
        sides = [(0, row - 1, row >= 1, -1, 1), (1, row + 1, row + 1 < rows, 1, 0)]

    def when(*conditions):
        conditions = [c for c in conditions if c is not None]
        if not conditions:
            return lambda body: body()
        return pl.when(functools.reduce(jnp.logical_and, conditions))

    def load(head):
        lanes = pl.ds(pl.multiple_of(head * HDIM, HDIM), HDIM)
        return [
            pltpu.make_async_copy(src.at[0, :, :, lanes], dst, load_sem.at[head, i])
            for i, (src, dst) in enumerate(
                (
                    (k_hbm, kv_all.at[0, head, 0]),
                    (v_hbm, kv_all.at[0, head, 1]),
                    (q_hbm, q_all.at[0, head]),
                )
            )
        ]

    def send_kv(side, head):
        slot, there, _, _, far_slot = side
        return remote(
            kv_all.at[0, head],
            kv_all.at[1 + far_slot, head],
            kv_send_sem.at[slot, head],
            kv_recv_sem.at[far_slot, head],
            {"space": there},
        )

    def got_kv(side, head):
        slot, there, _, _, _ = side
        return remote(
            kv_all.at[0, head],
            kv_all.at[1 + slot, head],
            kv_send_sem.at[slot, head],
            kv_recv_sem.at[slot, head],
            {"space": there},
        )

    def send_q(stage, head):
        return remote(
            q_all.at[stage, head],
            q_all.at[stage + 1, head],
            q_send_sem.at[stage, head],
            q_recv_sem.at[stage, head],
            {"tm": frame - 1},
        )

    def send_qb(stage):
        return remote(
            qb_all.at[stage],
            qb_all.at[stage + 1],
            q_send_sem.at[stage, heads],
            q_recv_sem.at[stage, heads],
            {"tm": frame - 1},
        )

    def send_o(dt, head):
        return remote(
            o_send.at[dt - 1, head],
            o_recv.at[dt - 1, head],
            o_send_sem.at[dt - 1, head],
            o_recv_sem.at[dt - 1, head],
            {"tm": frame + 1},
        )

    def each_head(body):
        def step(head, carry):
            body(head)
            return carry

        lax.fori_loop(0, heads, step, 0)

    partners = [({"space": side[1]}, side[2]) for side in sides] + [
        ({"tm": frame + 1}, has1),
        ({"tm": frame - 1}, prev1),
    ]
    barrier = pltpu.get_barrier_semaphore()
    for device, there in partners:

        @when(there)
        def _():
            pl.semaphore_signal(barrier, inc=1, device_id=device, device_id_type=MESH)

    @each_head
    def _(head):
        for copy in load(head):
            copy.start()

    lane = lax.broadcasted_iota(jnp.int32, (1, HDIM), 1)
    lane_row = lane // tile_cols
    lane_col = lane % tile_cols
    lane_dy = lane_row % 3 - 1
    row_ok = (row + lane_dy >= 0) & (row + lane_dy < rows) & (lane_row < 9)
    col_of = lax.broadcasted_iota(jnp.int32, (columns, 1), 0) // TILE
    table = jnp.zeros((columns, HDIM), jnp.float32)
    for col in range(tile_cols):
        dx = lane_col - col
        near = row_ok & (dx >= -1) & (dx <= 1)
        slot_of = lane_row * 3 + dx + 1
        picked = jnp.zeros((1, HDIM), jnp.int32)
        for slot in range(27):
            picked = jnp.where(slot_of == slot, win_ref[0, 0, col, slot], picked)
        allowed = near & ((picked == 1) | (slot_of == 4))
        offsets = jnp.where(allowed, 0.0, MASKED)
        table = jnp.where(col_of == col, offsets, table)
    qb_all[0] = table.astype(jnp.bfloat16)

    token = lax.broadcasted_iota(jnp.int32, (tokens, HDIM), 0)
    key_col = (token % columns) // TILE
    key_lane = lax.broadcasted_iota(jnp.int32, (tokens, HDIM), 1)
    for dt in range(3):
        for block, dy in enumerate([0] + [side[3] for side in sides]):
            hot = (dt * 3 + dy + 1) * tile_cols + key_col == key_lane
            kone[dt, pl.ds(block * tokens, tokens), :] = jnp.where(hot, 1.0, 0.0).astype(
                jnp.bfloat16
            )

    for side in sides:
        if side[2] is not None:

            @when(jnp.logical_not(side[2]))
            def _():
                @each_head
                def _(head):
                    kv_all[1 + side[0], head] = jnp.zeros(kv_all.shape[2:], jnp.bfloat16)

    peers = sum(
        1 if there is None else jnp.where(there, 1, 0).astype(jnp.int32) for _, there in partners
    )
    pl.semaphore_wait(barrier, peers)

    @when(prev1)
    def _():
        send_qb(0).start()

    @each_head
    def _(head):
        for copy in load(head):
            copy.wait()
        for side in sides:

            @when(side[2])
            def _():
                send_kv(side, head).start()

        @when(prev1, head < 2)
        def _():
            send_q(0, head).start()

    @when(has1)
    def _():
        send_qb(0).wait_recv()

        @when(prev1)
        def _():
            send_qb(1).start()

    blocks = range(1 + len(sides))

    def attend(dt, head):
        query = q_all[dt, head].reshape(tokens, HDIM)
        offsets = jnp.concatenate([qb_all[dt]] * TILE, axis=0)
        query = jnp.concatenate([query, offsets], axis=1)
        key = jnp.concatenate([kv_all[b, head, 0].reshape(tokens, HDIM) for b in blocks], axis=0)
        key = jnp.concatenate([key, kone[dt]], axis=1)
        value = jnp.concatenate([kv_all[b, head, 1].reshape(tokens, HDIM) for b in blocks], axis=0)
        scores = lax.dot_general(
            key, query, (((1,), (1,)), ((), ())), preferred_element_type=jnp.float32
        )
        top = jnp.max(scores, axis=0, keepdims=True)
        weights = jnp.exp2((scores - top) * EXP2_SCALE)
        total = jnp.sum(weights, axis=0, keepdims=True)
        part = lax.dot_general(
            value,
            weights.astype(jnp.bfloat16),
            (((0,), (0,)), ((), ())),
            preferred_element_type=jnp.float32,
        )
        return part / total, top * EXP2_SCALE + jnp.log2(total)

    extra_row = lax.broadcasted_iota(jnp.int32, (EXTRA, tokens), 0)

    def pack(dt, head, part, lse):
        high = lse.astype(jnp.bfloat16).astype(jnp.float32)
        middle = (lse - high).astype(jnp.bfloat16).astype(jnp.float32)
        low = lse - high - middle
        extra = jnp.where(extra_row == 0, high, jnp.where(extra_row == 1, middle, low))
        extra = jnp.where(extra_row < 3, extra, 0.0)
        o_send[dt - 1, head, pl.ds(0, HDIM), :] = part.astype(jnp.bfloat16)
        o_send[dt - 1, head, pl.ds(HDIM, EXTRA), :] = extra.astype(jnp.bfloat16)

    def unpack(dt, head):
        extra = o_recv[dt - 1, head, pl.ds(HDIM, EXTRA), :].astype(jnp.float32)
        part = o_recv[dt - 1, head, pl.ds(0, HDIM), :].astype(jnp.float32)
        return part, jnp.sum(extra, axis=0, keepdims=True)

    def keep(dt, head):
        part, lse = attend(dt, head)
        o_own[dt, head] = part
        lse_own[dt, head] = jnp.broadcast_to(lse, lse_own.shape[2:])

    def kept(dt, head):
        return o_own[dt, head], lse_own[dt, head][:1]

    def merge(one, two):
        top = jnp.maximum(one[1], two[1])
        share_one, share_two = jnp.exp2(one[1] - top), jnp.exp2(two[1] - top)
        total = share_one + share_two
        part = one[0] * (share_one / total) + two[0] * (share_two / total)
        return part, top + jnp.log2(total)

    def finish(head, part):
        lanes = pl.ds(pl.multiple_of(head * HDIM, HDIM), HDIM)
        out_ref[0, :, :, lanes] = part.T.astype(jnp.bfloat16).reshape(TILE, columns, HDIM)

    def step(i, carry):
        far, passing, last = i - FAR_LAG, i - PASS_LAG, i - LAST_LAG
        in_far = (far >= 0) & (far < heads)
        in_passing = (passing >= 0) & (passing < heads)
        in_last = (last >= 0) & (last < heads)

        @when(i < heads)
        def _():
            @when(has1)
            def _():
                send_q(0, i).wait_recv()

                @when(prev1)
                def _():
                    send_q(1, i).start()

            @when(prev1, i + 2 < heads)
            def _():
                send_q(0, i + 2).start()

            for side in sides:

                @when(side[2])
                def _():
                    got_kv(side, i).wait_recv()

            @when(has1)
            def _():
                keep(1, i)

        @when(in_far, has2)
        def _():
            @when(far == 0)
            def _():
                send_qb(1).wait_recv()

            send_q(1, far).wait_recv()
            pack(2, far, *attend(2, far))

        @when(in_passing, has1)
        def _():
            @when(prev1)
            def _():
                send_o(2, passing).wait_recv()
                pack(1, passing, *merge(kept(1, passing), unpack(2, passing)))

            @when(jnp.logical_not(prev1))
            def _():
                pack(1, passing, *kept(1, passing))

        @when(i < heads)
        def _():
            keep(0, i)

        @when(in_far, has2)
        def _():
            send_o(2, far).start()

        @when(in_passing, has1)
        def _():
            send_o(1, passing).start()

        @when(in_last)
        def _():
            @when(prev1)
            def _():
                send_o(1, last).wait_recv()
                finish(last, merge(kept(0, last), unpack(1, last))[0])

            @when(jnp.logical_not(prev1))
            def _():
                finish(last, o_own[0, last])

        return carry

    lax.fori_loop(0, heads + LAST_LAG, step, 0)

    @when(prev1)
    def _():
        send_qb(0).wait_send()

        @when(has1)
        def _():
            send_qb(1).wait_send()

    @each_head
    def _(head):
        for side in sides:

            @when(side[2])
            def _():
                send_kv(side, head).wait_send()

        @when(prev1)
        def _():
            send_q(0, head).wait_send()

            @when(has1)
            def _():
                send_q(1, head).wait_send()

        @when(has1)
        def _():
            send_o(1, head).wait_send()

        @when(has2)
        def _():
            send_o(2, head).wait_send()


def solution(mesh):
    frames, rows = mesh.shape["tm"], mesh.shape["space"]

    def on_device(queries, keys, values, window):
        _, _, columns, channels = queries.shape
        heads = channels // HDIM
        tokens = TILE * columns
        beside = min(rows - 1, 2)
        block = (TILE, columns, HDIM)
        dma = pltpu.SemaphoreType.DMA
        return pl.pallas_call(
            functools.partial(kernel, frames, rows),
            out_shape=jax.ShapeDtypeStruct(queries.shape, jnp.bfloat16),
            in_specs=[pl.BlockSpec(memory_space=pl.ANY)] * 3
            + [pl.BlockSpec(memory_space=pltpu.SMEM)],
            out_specs=pl.BlockSpec(memory_space=pltpu.VMEM),
            scratch_shapes=[
                pltpu.VMEM((3, heads, *block), jnp.bfloat16),
                pltpu.VMEM((1 + beside, heads, 2, *block), jnp.bfloat16),
                pltpu.VMEM((3, columns, HDIM), jnp.bfloat16),
                pltpu.VMEM((3, (1 + beside) * tokens, HDIM), jnp.bfloat16),
                pltpu.VMEM((2, heads, HDIM + EXTRA, tokens), jnp.bfloat16),
                pltpu.VMEM((2, heads, HDIM + EXTRA, tokens), jnp.bfloat16),
                pltpu.VMEM((2, heads, HDIM, tokens), jnp.float32),
                pltpu.VMEM((2, heads, 8, tokens), jnp.float32),
                dma((heads, 3)),
                dma((max(beside, 1), heads)),
                dma((max(beside, 1), heads)),
                dma((2, heads + 1)),
                dma((2, heads + 1)),
                dma((2, heads)),
                dma((2, heads)),
            ],
            compiler_params=pltpu.CompilerParams(collective_id=0, has_side_effects=True),
        )(queries, keys, values, window)

    placed = P(("group", "tm"), "space", None, "head")
    return jax.shard_map(
        on_device,
        mesh=mesh,
        in_specs=(placed, placed, placed, P(("group", "tm"), "space", None, None)),
        out_specs=placed,
        check_vma=False,
    )
```

profile of v0, /device:TPU:24, one launch (start us, length us, event | category | flops | bytes accessed | tf_op | source)
XLA Modules:
  0.0 56.3 jit_solution(13464884629358077955)
XLA Ops:
  0.0 54.2 %shard_map.46 = bf16[1,8,32,1536]{3,2,1,0:T(8,128)(2,1)} custom-call(bf16[1,8,32,1536]{3,2,1,0:T(8,128)(2,1)} %q_hbm.1, bf16[1,8,32,1536]{3,2,1,0:T(8,128)(2,1)} %k_hbm.1, bf16[1,8,32,1536]{3,2,1,0:T(8,128)(2,1)} %v_hbm.1, s32[1,1,4,27]{3,2,1,0:T(4,128)} %win_ref.1), custom_call_target="tpu_custom_call" | custom-call | tf_op jit(solution)/shard_map/pallas_call | solution.py:407
  54.2 2.1 %copy.6 = bf16[1,8,32,1536]{3,2,1,0:T(8,128)(2,1)} copy(bf16[1,8,32,1536]{3,2,1,0:T(8,128)(2,1)} %shard_map.46) | data formatting | bytes 1572864
where the time goes:
time: 56.8 us; the launch traced here: 56.3 us
  Pallas kernels  54.2 us (95%)
  local copies, waits for them, and re-layouts  2.06 us (4%)
    pallas_call x1, Pallas kernels, on_device(): pl.pallas_call(functools.partial(kernel, frames, rows), out_shape=jax.Sha...  54.2 us
    unnamed x1, local copies, waits for them, and re-layouts  2.06 us

commit v1 on v0

--- a/solution.py
+++ b/solution.py
@@ -10,10 +10,12 @@
 
 HDIM = 128
 TILE = 8
-EXTRA = 8
-FAR_LAG, PASS_LAG, LAST_LAG = 1, 3, 5
+LANES = 128
+OWN_AHEAD = 3
+FAR_LAG, PASS_LAG, LAST_LAG = 1, 2, 5
 MASKED = -float(2**17)
 EXP2_SCALE = HDIM ** (-0.5) * math.log2(math.e)
+VMEM_LIMIT = 40 * 2**20
 MESH = pl.DeviceIdType.MESH
 
 
@@ -34,7 +36,7 @@
     q_hbm,
     k_hbm,
     v_hbm,
-    win_ref,
+    win_hbm,
     out_ref,
     q_all,
     kv_all,
@@ -44,7 +46,9 @@
     o_recv,
     o_own,
     lse_own,
+    win_ref,
     load_sem,
+    win_sem,
     kv_send_sem,
     kv_recv_sem,
     q_send_sem,
@@ -152,11 +156,43 @@
         def _():
             pl.semaphore_signal(barrier, inc=1, device_id=device, device_id_type=MESH)
 
-    @each_head
-    def _(head):
+    window = pltpu.make_async_copy(win_hbm, win_ref, win_sem)
+    for copy in load(0):
+        copy.start()
+    window.start()
+
+    def load_rest(head, carry):
         for copy in load(head):
             copy.start()
-
+        return carry
+
+    lax.fori_loop(1, heads, load_rest, 0)
+
+    peers = sum(
+        1 if there is None else jnp.where(there, 1, 0).astype(jnp.int32) for _, there in partners
+    )
+    pl.semaphore_wait(barrier, peers)
+
+    def launch(head, own):
+        for copy in load(head):
+            copy.wait()
+        for side in sides:
+
+            @when(side[2])
+            def _():
+                send_kv(side, head).start()
+
+        if own:
+
+            @when(prev1)
+            def _():
+                send_q(0, head).start()
+
+    ahead = min(OWN_AHEAD, heads)
+    for head in range(ahead):
+        launch(head, True)
+
+    window.wait()
     lane = lax.broadcasted_iota(jnp.int32, (1, HDIM), 1)
     lane_row = lane // tile_cols
     lane_col = lane % tile_cols
@@ -176,6 +212,16 @@
         table = jnp.where(col_of == col, offsets, table)
     qb_all[0] = table.astype(jnp.bfloat16)
 
+    @when(prev1)
+    def _():
+        send_qb(0).start()
+
+    def launch_rest(head, carry):
+        launch(head, False)
+        return carry
+
+    lax.fori_loop(ahead, heads, launch_rest, 0)
+
     token = lax.broadcasted_iota(jnp.int32, (tokens, HDIM), 0)
     key_col = (token % columns) // TILE
     key_lane = lax.broadcasted_iota(jnp.int32, (tokens, HDIM), 1)
@@ -195,37 +241,6 @@
                 def _(head):
                     kv_all[1 + side[0], head] = jnp.zeros(kv_all.shape[2:], jnp.bfloat16)
 
-    peers = sum(
-        1 if there is None else jnp.where(there, 1, 0).astype(jnp.int32) for _, there in partners
-    )
-    pl.semaphore_wait(barrier, peers)
-
-    @when(prev1)
-    def _():
-        send_qb(0).start()
-
-    @each_head
-    def _(head):
-        for copy in load(head):
-            copy.wait()
-        for side in sides:
-
-            @when(side[2])
-            def _():
-                send_kv(side, head).start()
-
-        @when(prev1, head < 2)
-        def _():
-            send_q(0, head).start()
-
-    @when(has1)
-    def _():
-        send_qb(0).wait_recv()
-
-        @when(prev1)
-        def _():
-            send_qb(1).start()
-
     blocks = range(1 + len(sides))
 
     def attend(dt, head):
@@ -249,24 +264,33 @@
         )
         return part / total, top * EXP2_SCALE + jnp.log2(total)
 
-    extra_row = lax.broadcasted_iota(jnp.int32, (EXTRA, tokens), 0)
+    chunks = tokens // LANES
+    extra_row = lax.broadcasted_iota(jnp.int32, (o_send.shape[2] - chunks * HDIM, LANES), 0)
 
     def pack(dt, head, part, lse):
         high = lse.astype(jnp.bfloat16).astype(jnp.float32)
         middle = (lse - high).astype(jnp.bfloat16).astype(jnp.float32)
         low = lse - high - middle
-        extra = jnp.where(extra_row == 0, high, jnp.where(extra_row == 1, middle, low))
-        extra = jnp.where(extra_row < 3, extra, 0.0)
-        o_send[dt - 1, head, pl.ds(0, HDIM), :] = part.astype(jnp.bfloat16)
-        o_send[dt - 1, head, pl.ds(HDIM, EXTRA), :] = extra.astype(jnp.bfloat16)
+        extra = jnp.zeros(extra_row.shape, jnp.float32)
+        for chunk in range(chunks):
+            lanes = slice(chunk * LANES, (chunk + 1) * LANES)
+            o_send[dt - 1, head, pl.ds(chunk * HDIM, HDIM), :] = part[:, lanes].astype(jnp.bfloat16)
+            for word, values in enumerate((high, middle, low)):
+                extra = jnp.where(extra_row == chunk * 3 + word, values[:, lanes], extra)
+        o_send[dt - 1, head, pl.ds(chunks * HDIM, extra_row.shape[0]), :] = extra.astype(
+            jnp.bfloat16
+        )
 
     def unpack(dt, head):
-        extra = o_recv[dt - 1, head, pl.ds(HDIM, EXTRA), :].astype(jnp.float32)
-        part = o_recv[dt - 1, head, pl.ds(0, HDIM), :].astype(jnp.float32)
-        return part, jnp.sum(extra, axis=0, keepdims=True)
-
-    def keep(dt, head):
-        part, lse = attend(dt, head)
+        extra = o_recv[dt - 1, head, pl.ds(chunks * HDIM, extra_row.shape[0]), :].astype(jnp.float32)
+        parts, lses = [], []
+        for chunk in range(chunks):
+            parts.append(o_recv[dt - 1, head, pl.ds(chunk * HDIM, HDIM), :].astype(jnp.float32))
+            first = chunk * 3
+            lses.append(extra[first : first + 1] + extra[first + 1 : first + 2] + extra[first + 2 : first + 3])
+        return jnp.concatenate(parts, axis=1), jnp.concatenate(lses, axis=1)
+
+    def keep(dt, head, part, lse):
         o_own[dt, head] = part
         lse_own[dt, head] = jnp.broadcast_to(lse, lse_own.shape[2:])
 
@@ -284,26 +308,45 @@
         lanes = pl.ds(pl.multiple_of(head * HDIM, HDIM), HDIM)
         out_ref[0, :, :, lanes] = part.T.astype(jnp.bfloat16).reshape(TILE, columns, HDIM)
 
+    def relay(head):
+        @when(has1, head < heads)
+        def _():
+            send_q(0, head).wait_recv()
+
+            @when(prev1)
+            def _():
+                send_q(1, head).start()
+
+    def inside(head):
+        return (head >= 0) & (head < heads)
+
+    relay(jnp.int32(0))
+
+    @when(has1)
+    def _():
+        send_qb(0).wait_recv()
+
+        @when(prev1)
+        def _():
+            send_qb(1).start()
+
     def step(i, carry):
         far, passing, last = i - FAR_LAG, i - PASS_LAG, i - LAST_LAG
-        in_far = (far >= 0) & (far < heads)
-        in_passing = (passing >= 0) & (passing < heads)
-        in_last = (last >= 0) & (last < heads)
+
+        @when(inside(far), has2)
+        def _():
+            @when(far == 0)
+            def _():
+                send_qb(1).wait_recv()
+
+            send_q(1, far).wait_recv()
+            pack(2, far, *attend(2, far))
+            send_o(2, far).start()
+
+        relay(i + 1)
 
         @when(i < heads)
         def _():
-            @when(has1)
-            def _():
-                send_q(0, i).wait_recv()
-
-                @when(prev1)
-                def _():
-                    send_q(1, i).start()
-
-            @when(prev1, i + 2 < heads)
-            def _():
-                send_q(0, i + 2).start()
-
             for side in sides:
 
                 @when(side[2])
@@ -312,18 +355,9 @@
 
             @when(has1)
             def _():
-                keep(1, i)
-
-        @when(in_far, has2)
-        def _():
-            @when(far == 0)
-            def _():
-                send_qb(1).wait_recv()
-
-            send_q(1, far).wait_recv()
-            pack(2, far, *attend(2, far))
-
-        @when(in_passing, has1)
+                keep(1, i, *attend(1, i))
+
+        @when(inside(passing), has1)
         def _():
             @when(prev1)
             def _():
@@ -334,19 +368,17 @@
             def _():
                 pack(1, passing, *kept(1, passing))
 
+            send_o(1, passing).start()
+
         @when(i < heads)
         def _():
-            keep(0, i)
-
-        @when(in_far, has2)
-        def _():
-            send_o(2, far).start()
-
-        @when(in_passing, has1)
-        def _():
-            send_o(1, passing).start()
-
-        @when(in_last)
+            keep(0, i, *attend(0, i))
+
+        @when(prev1, i + ahead < heads)
+        def _():
+            send_q(0, i + ahead).start()
+
+        @when(inside(last))
         def _():
             @when(prev1)
             def _():
@@ -403,23 +435,26 @@
         tokens = TILE * columns
         beside = min(rows - 1, 2)
         block = (TILE, columns, HDIM)
+        chunks = tokens // LANES
+        packed = chunks * HDIM + -(-3 * chunks // 8) * 8
         dma = pltpu.SemaphoreType.DMA
         return pl.pallas_call(
             functools.partial(kernel, frames, rows),
             out_shape=jax.ShapeDtypeStruct(queries.shape, jnp.bfloat16),
-            in_specs=[pl.BlockSpec(memory_space=pl.ANY)] * 3
-            + [pl.BlockSpec(memory_space=pltpu.SMEM)],
+            in_specs=[pl.BlockSpec(memory_space=pl.ANY)] * 4,
             out_specs=pl.BlockSpec(memory_space=pltpu.VMEM),
             scratch_shapes=[
                 pltpu.VMEM((3, heads, *block), jnp.bfloat16),
                 pltpu.VMEM((1 + beside, heads, 2, *block), jnp.bfloat16),
                 pltpu.VMEM((3, columns, HDIM), jnp.bfloat16),
                 pltpu.VMEM((3, (1 + beside) * tokens, HDIM), jnp.bfloat16),
-                pltpu.VMEM((2, heads, HDIM + EXTRA, tokens), jnp.bfloat16),
-                pltpu.VMEM((2, heads, HDIM + EXTRA, tokens), jnp.bfloat16),
+                pltpu.VMEM((2, heads, packed, LANES), jnp.bfloat16),
+                pltpu.VMEM((2, heads, packed, LANES), jnp.bfloat16),
                 pltpu.VMEM((2, heads, HDIM, tokens), jnp.float32),
                 pltpu.VMEM((2, heads, 8, tokens), jnp.float32),
+                pltpu.SMEM(window.shape, jnp.int32),
                 dma((heads, 3)),
+                dma,
                 dma((max(beside, 1), heads)),
                 dma((max(beside, 1), heads)),
                 dma((2, heads + 1)),
@@ -427,8 +462,10 @@
                 dma((2, heads)),
                 dma((2, heads)),
             ],
-            compiler_params=pltpu.CompilerParams(collective_id=0, has_side_effects=True),
-        )(queries, keys, values, window)
+            compiler_params=pltpu.CompilerParams(
+                collective_id=0, has_side_effects=True, vmem_limit_bytes=VMEM_LIMIT
+            ),
+        )(*[pltpu.with_memory_space_constraint(a, pltpu.HBM) for a in (queries, keys, values, window)])
 
     placed = P(("group", "tm"), "space", None, "head")
     return jax.shard_map(

time: 56.8 us -> 51.5 us (0.907)
  Pallas kernels: 54.2 us -> 50.2 us
  local copies, waits for them, and re-layouts: 2.06 us -> 0.88 us
    pallas_call x1, Pallas kernels: 54.2 us -> 50.2 us  [on_device(): pl.pallas_call(functools.partial(kernel, frames, rows), out_shape=jax.Sha...]
    unnamed x1, local copies, waits for them, and re-layouts: 2.06 us -> 0.88 us
where the time goes in v1:
time: 51.5 us; the launch traced here: 51.1 us
  Pallas kernels  50.2 us (97%)
  local copies, waits for them, and re-layouts  0.88 us (2%)
    pallas_call x1, Pallas kernels, on_device(): pl.pallas_call(functools.partial(kernel, frames, rows), out_shape=jax.Sha...  50.2 us

profile of v1, /device:TPU:24, one launch (start us, length us, event | category | flops | bytes accessed | tf_op | source)
XLA Modules:
  0.0 51.1 jit_solution(3831080281617100308)
XLA Ops:
  0.0 50.2 %shard_map.46 = bf16[1,8,32,1536]{3,2,1,0:T(8,128)(2,1)S(1)} custom-call(bf16[1,8,32,1536]{3,2,1,0:T(8,128)(2,1)} %q_hbm.1, bf16[1,8,32,1536]{3,2,1,0:T(8,128)(2,1)} %k_hbm.1, bf16[1,8,32,1536]{3,2,1,0:T(8,128)(2,1)} %v_hbm.1, s32[1,1,4,27]{3,2,1,0:T(4,128)} %win_hbm.1), custom_call_target="tpu_custom_call" | custom-call | tf_op jit(solution)/shard_map/pallas_call | solution.py:441
  50.3 0.9 %copy.6 = bf16[1,8,32,1536]{3,2,1,0:T(8,128)(2,1)} copy(bf16[1,8,32,1536]{3,2,1,0:T(8,128)(2,1)S(1)} %shard_map.46) | data formatting | bytes 1572864

commit v2 on v1

v2 whole, which is shorter than its diff:
```python
import functools
import math

import jax
import jax.numpy as jnp
from jax import lax
from jax.experimental import pallas as pl
from jax.experimental.pallas import tpu as pltpu
from jax.sharding import PartitionSpec as P

HDIM = 128
TILE = 8
PARTS = 1
EARLY = 1
SHIFT = 0
DIRECT = 0
OWN_LAG, RELAY_LAG, KV_LAG, FAR_LAG, NEAR_LAG = -3, -1, 1, 1, 1
MERGE_LAG, EARLY_LAG, HOME_LAG, LAST_LAG = 2, 1, 1, 5
FORWARD_AT = 0
MASKED = -float(2**17)
EXP2_SCALE = HDIM ** (-0.5) * math.log2(math.e)
VMEM_LIMIT = 40 * 2**20
MESH = pl.DeviceIdType.MESH


def remote(src, dst, send_sem, recv_sem, device):
    return pltpu.make_async_remote_copy(
        src_ref=src,
        dst_ref=dst,
        send_sem=send_sem,
        recv_sem=recv_sem,
        device_id=device,
        device_id_type=MESH,
    )


def kernel(
    frames,
    rows,
    shift,
    q_hbm,
    k_hbm,
    v_hbm,
    win_hbm,
    out_ref,
    q_all,
    kv_all,
    kv_before,
    qb_all,
    kone,
    o_send,
    o_recv,
    lse_send,
    lse_recv,
    o_own,
    lse_own,
    back_send,
    back_recv,
    win_ref,
    ready_sem,
    load_sem,
    win_sem,
    kv_send_sem,
    kv_recv_sem,
    before_send_sem,
    before_recv_sem,
    q_send_sem,
    q_recv_sem,
    qb_send_sem,
    qb_recv_sem,
    o_send_sem,
    o_recv_sem,
    give_send_sem,
    give_recv_sem,
    back_send_sem,
    back_recv_sem,
):
    frame = lax.axis_index("tm")
    row = lax.axis_index("space")
    core = lax.axis_index("head")
    slots = q_all.shape[1]
    heads = slots - shift
    columns = kv_all.shape[4]
    width = columns // PARTS
    span = TILE * width
    tile_cols = columns // TILE
    tokens = TILE * columns
    count = heads + shift * (2 * core - 1) if shift else heads
    has1 = frame + 1 < frames
    has2 = frame + 2 < frames
    prev1 = frame >= 1
    if rows == 1:
        sides = []
    elif rows == 2:
        sides = [(0, 1 - row, None, 1 - 2 * row, 0)]
    else:
        sides = [(0, row - 1, row >= 1, -1, 1), (1, row + 1, row + 1 < rows, 1, 0)]
    blocks = range(1 + len(sides))

    def when(*conditions):
        conditions = [c for c in conditions if c is not None]
        if not conditions:
            return lambda body: body()
        return pl.when(functools.reduce(jnp.logical_and, conditions))

    def lanes_of(head):
        start = head * HDIM
        return pl.ds(start if isinstance(head, int) else pl.multiple_of(start, HDIM), HDIM)

    def pieces(head, slot):
        lanes = lanes_of(head)
        halves = [
            (q_hbm.at[0, :, pl.ds(part * width, width), lanes], q_all.at[0, slot, part])
            for part in range(PARTS)
        ]
        return [
            (k_hbm.at[0, :, :, lanes], kv_all.at[0, slot, 0]),
            (v_hbm.at[0, :, :, lanes], kv_all.at[0, slot, 1]),
        ] + halves

    def load(slot):
        return [
            pltpu.make_async_copy(src, dst, load_sem.at[slot, i])
            for i, (src, dst) in enumerate(pieces(slot, slot))
        ]

    def give(extra):
        return [
            remote(
                src, dst, give_send_sem.at[extra, i], give_recv_sem.at[extra, i], {"head": 1 - core}
            )
            for i, (src, dst) in enumerate(pieces(heads - shift + extra, heads + extra))
        ]

    def give_back(extra):
        return remote(
            back_send.at[extra],
            back_recv.at[extra],
            back_send_sem.at[extra],
            back_recv_sem.at[extra],
            {"head": 1 - core},
        )

    def send_kv(side, slot):
        index, there, _, _, far_index = side
        return remote(
            kv_all.at[0, slot],
            kv_all.at[1 + far_index, slot],
            kv_send_sem.at[index, slot],
            kv_recv_sem.at[far_index, slot],
            {"space": there},
        )

    def got_kv(side, slot):
        index, there, _, _, _ = side
        return remote(
            kv_all.at[0, slot],
            kv_all.at[1 + index, slot],
            kv_send_sem.at[index, slot],
            kv_recv_sem.at[index, slot],
            {"space": there},
        )

    def forward(block, slot):
        return remote(
            kv_all.at[block, slot],
            kv_before.at[block, slot],
            before_send_sem.at[block, slot],
            before_recv_sem.at[block, slot],
            {"tm": frame + 1},
        )

    def send_q(stage, slot, part):
        return remote(
            q_all.at[stage, slot, part],
            q_all.at[stage + 1, slot, part],
            q_send_sem.at[stage, slot, part],
            q_recv_sem.at[stage, slot, part],
            {"tm": frame - 1},
        )

    def send_qb(stage):
        return remote(
            qb_all.at[stage],
            qb_all.at[stage + 1],
            qb_send_sem.at[stage],
            qb_recv_sem.at[stage],
            {"tm": frame - 1},
        )

    def send_o(dt, slot, part, hops=1):
        pairs = ((o_send, o_recv), (lse_send, lse_recv))
        return [
            remote(
                src.at[dt - 1, slot, part],
                dst.at[dt - 1, slot, part],
                o_send_sem.at[dt - 1, slot, part, i],
                o_recv_sem.at[dt - 1, slot, part, i],
                {"tm": frame + hops},
            )
            for i, (src, dst) in enumerate(pairs)
        ]

    def each_slot(body, first=0):
        def step(slot, carry):
            body(slot)
            return carry

        lax.fori_loop(first, count, step, 0)

    partners = [({"space": side[1]}, side[2]) for side in sides]
    if shift:
        partners.append(({"head": 1 - core}, None))
    barrier = pltpu.get_barrier_semaphore()
    for device, there in partners + [({"tm": frame + 1}, has1)]:

        @when(there)
        def _():
            pl.semaphore_signal(barrier, inc=1, device_id=device, device_id_type=MESH)

    window = pltpu.make_async_copy(win_hbm, win_ref, win_sem)
    for slot in range(EARLY + 1):
        for copy in load(slot):
            copy.start()
    window.start()

    def is_local(slot):
        return slot < heads if shift else None

    @functools.partial(each_slot, first=EARLY + 1)
    def _(slot):
        @when(is_local(slot))
        def _():
            for copy in load(slot):
                copy.start()

    peers = sum(
        1 if there is None else jnp.where(there, 1, 0).astype(jnp.int32)
        for there in [there for _, there in partners] + [prev1]
    )
    pl.semaphore_wait(barrier, peers)

    @when(prev1)
    def _():
        pl.semaphore_signal(ready_sem, inc=1, device_id={"tm": frame - 1}, device_id_type=MESH)

    def send_rows(slot):
        for side in sides:

            @when(side[2])
            def _():
                send_kv(side, slot).start()

    def launch(slot):
        for copy in load(slot):
            copy.wait()
        send_rows(slot)

    own_ahead = -OWN_LAG
    first_rest = EARLY + -(-own_ahead // PARTS)

    def send_own(slot):
        @when(prev1)
        def _():
            for part in range(PARTS):
                if (slot - EARLY) * PARTS + part < own_ahead:
                    send_q(0, slot, part).start()

    for slot in range(EARLY + 1):
        launch(slot)
    send_own(EARLY)

    window.wait()
    lane = lax.broadcasted_iota(jnp.int32, (1, HDIM), 1)
    lane_row = lane // tile_cols
    lane_col = lane % tile_cols
    lane_dy = lane_row % 3 - 1
    row_ok = (row + lane_dy >= 0) & (row + lane_dy < rows) & (lane_row < 9)
    col_of = lax.broadcasted_iota(jnp.int32, (columns, 1), 0) // TILE
    table = jnp.zeros((columns, HDIM), jnp.float32)
    for col in range(tile_cols):
        dx = lane_col - col
        near = row_ok & (dx >= -1) & (dx <= 1)
        slot_of_lane = lane_row * 3 + dx + 1
        picked = jnp.zeros((1, HDIM), jnp.int32)
        for slot in range(27):
            picked = jnp.where(slot_of_lane == slot, win_ref[0, 0, col, slot], picked)
        allowed = near & ((picked == 1) | (slot_of_lane == 4))
        offsets = jnp.where(allowed, 0.0, MASKED)
        table = jnp.where(col_of == col, offsets, table)
    for part in range(PARTS):
        qb_all[0, part] = table[part * width : (part + 1) * width].astype(jnp.bfloat16)

    @when(prev1)
    def _():
        send_qb(0).start()

    for slot in range(EARLY + 1, first_rest):
        launch(slot)
        send_own(slot)

    @when(has1)
    def _():
        pl.semaphore_wait(ready_sem, 1)

    @when(has2)
    def _():
        for slot in range(EARLY):
            forward(0, slot).start()

    if shift:

        @when(core == 0)
        def _():
            for extra in range(shift):
                for copy in give(extra):
                    copy.start()

    @functools.partial(each_slot, first=first_rest)
    def _(slot):
        @when(is_local(slot))
        def _():
            for copy in load(slot):
                copy.wait()

        if shift:
            for extra in range(shift):

                @when(slot == heads + extra)
                def _():
                    for copy in give(extra):
                        copy.wait_recv()

        send_rows(slot)

    token = lax.broadcasted_iota(jnp.int32, (tokens, HDIM), 0)
    key_col = (token % columns) // TILE
    key_lane = lax.broadcasted_iota(jnp.int32, (tokens, HDIM), 1)
    for dt in range(3):
        for block, dy in enumerate([0] + [side[3] for side in sides]):
            hot = (dt * 3 + dy + 1) * tile_cols + key_col == key_lane
            kone[dt, pl.ds(block * tokens, tokens), :] = jnp.where(hot, 1.0, 0.0).astype(
                jnp.bfloat16
            )

    for side in sides:
        if side[2] is not None:

            @when(jnp.logical_not(side[2]))
            def _():
                @each_slot
                def _(slot):
                    kv_all[1 + side[0], slot] = jnp.zeros(kv_all.shape[2:], jnp.bfloat16)

                for slot in range(EARLY):
                    kv_before[1 + side[0], slot] = jnp.zeros(kv_before.shape[2:], jnp.bfloat16)

    def attend(stage, dt, slot, part, source):
        query = q_all[stage, slot, part].reshape(span, HDIM)
        offsets = jnp.concatenate([qb_all[stage, part]] * TILE, axis=0)
        query = jnp.concatenate([query, offsets], axis=1)
        key = jnp.concatenate([source[b, slot, 0].reshape(tokens, HDIM) for b in blocks], axis=0)
        key = jnp.concatenate([key, kone[dt]], axis=1)
        value = jnp.concatenate([source[b, slot, 1].reshape(tokens, HDIM) for b in blocks], axis=0)
        scores = lax.dot_general(
            key, query, (((1,), (1,)), ((), ())), preferred_element_type=jnp.float32
        )
        top = jnp.max(scores, axis=0, keepdims=True)
        weights = jnp.exp2((scores - top) * EXP2_SCALE)
        total = jnp.sum(weights, axis=0, keepdims=True)
        part_out = lax.dot_general(
            value,
            weights.astype(jnp.bfloat16),
            (((0,), (0,)), ((), ())),
            preferred_element_type=jnp.float32,
        )
        return part_out / total, top * EXP2_SCALE + jnp.log2(total)

    def pack(dt, slot, part, result, straight=None):
        o_send[dt - 1, slot, part] = result[0].astype(jnp.bfloat16)
        lse_send[dt - 1, slot, part] = result[1]

        @when(None if straight is None else jnp.logical_not(straight))
        def _():
            for copy in send_o(dt, slot, part):
                copy.start()

        if straight is not None:

            @when(straight)
            def _():
                for copy in send_o(dt, slot, part, 2):
                    copy.start()

    def unpack(dt, slot, part):
        for copy in send_o(dt, slot, part):
            copy.wait_recv()
        return o_recv[dt - 1, slot, part].astype(jnp.float32), lse_recv[dt - 1, slot, part]

    def keep(dt, slot, part, result):
        o_own[dt, slot, part] = result[0]
        lse_own[dt, slot, part] = result[1]

    def kept(dt, slot, part):
        return o_own[dt, slot, part], lse_own[dt, slot, part]

    def merge(one, two):
        top = jnp.maximum(one[1], two[1])
        share_one, share_two = jnp.exp2(one[1] - top), jnp.exp2(two[1] - top)
        total = share_one + share_two
        mixed = one[0] * (share_one / total) + two[0] * (share_two / total)
        return mixed, top + jnp.log2(total)

    def finish(slot, part, value):
        done = value.T.astype(jnp.bfloat16).reshape(TILE, width, HDIM)
        here = pl.ds(part * width, width)

        @when(is_local(slot))
        def _():
            out_ref[0, :, here, lanes_of(slot)] = done

        for extra in range(shift):

            @when(slot == heads + extra)
            def _():
                back_send[extra, :, here, :] = done
                if part == PARTS - 1:
                    give_back(extra).start()

    def inside(place):
        return (place >= 0) & (place < count)

    def is_early(place):
        return place >= count - EARLY

    def is_direct(place):
        return (place >= count - EARLY - DIRECT) & (place < count - EARLY)

    def slot_at(place):
        return jnp.where(is_early(place), place - (count - EARLY), place + EARLY)

    def relay(place, part):
        @when(has1, inside(place))
        def _():
            slot = slot_at(place)
            send_q(0, slot, part).wait_recv()

            @when(prev1, jnp.logical_not(is_early(place)))
            def _():
                send_q(1, slot, part).start()

    for n in range(-RELAY_LAG):
        relay(jnp.int32(n // PARTS), n % PARTS)

    @when(has1)
    def _():
        send_qb(0).wait_recv()

        @when(prev1)
        def _():
            send_qb(1).start()

    def step(i, carry):
        for g in range(PARTS):

            def at(lag):
                place = i + (g - lag) // PARTS
                return place, slot_at(place), (g - lag) % PARTS

            @when(i * PARTS + g == FORWARD_AT)
            def _():
                for slot in range(EARLY):
                    for side in sides:

                        @when(side[2])
                        def _():
                            got_kv(side, slot).wait_recv()

                            @when(has2)
                            def _():
                                forward(1 + side[0], slot).start()

            place, slot, part = at(KV_LAG)
            if part == 0:

                @when(inside(place), jnp.logical_not(is_early(place)))
                def _():
                    for side in sides:

                        @when(side[2])
                        def _():
                            got_kv(side, slot).wait_recv()

            place, slot, part = at(FAR_LAG)

            @when(inside(place), has2, jnp.logical_not(is_early(place)))
            def _():
                if part == 0:

                    @when(place == 0)
                    def _():
                        send_qb(1).wait_recv()

                send_q(1, slot, part).wait_recv()
                pack(2, slot, part, attend(2, 2, slot, part, kv_all), is_direct(place))

            relay(*at(RELAY_LAG)[::2])

            place, slot, part = at(NEAR_LAG)

            @when(inside(place), has1)
            def _():
                keep(1, slot, part, attend(1, 1, slot, part, kv_all))

            place, slot, part = at(MERGE_LAG)

            @when(inside(place), has1, jnp.logical_not(is_early(place)))
            def _():
                joins = prev1 & jnp.logical_not(is_direct(place))

                @when(joins)
                def _():
                    pack(1, slot, part, merge(kept(1, slot, part), unpack(2, slot, part)))

                @when(jnp.logical_not(joins))
                def _():
                    pack(1, slot, part, kept(1, slot, part))

            place, slot, part = at(EARLY_LAG)

            @when(inside(place), has1, is_early(place))
            def _():
                @when(prev1)
                def _():
                    if part == 0:
                        got_before(slot)
                    before = attend(1, 2, slot, part, kv_before)
                    pack(1, slot, part, merge(kept(1, slot, part), before))

                @when(jnp.logical_not(prev1))
                def _():
                    pack(1, slot, part, kept(1, slot, part))

            place, slot, part = at(HOME_LAG)

            @when(inside(place))
            def _():
                keep(0, slot, part, attend(0, 0, slot, part, kv_all))

            place, slot, part = at(OWN_LAG)

            @when(prev1, inside(place))
            def _():
                send_q(0, slot, part).start()

            place, slot, part = at(LAST_LAG)

            @when(inside(place))
            def _():
                joins = (frame >= 2) & is_direct(place)

                @when(prev1, jnp.logical_not(joins))
                def _():
                    merged = merge(kept(0, slot, part), unpack(1, slot, part))
                    finish(slot, part, merged[0])

                @when(joins)
                def _():
                    merged = merge(kept(0, slot, part), unpack(1, slot, part))
                    merged = merge(merged, unpack(2, slot, part))
                    finish(slot, part, merged[0])

                @when(jnp.logical_not(prev1))
                def _():
                    finish(slot, part, o_own[0, slot, part])

        return carry

    def got_before(slot):
        forward(0, slot).wait_recv()
        for side in sides:

            @when(side[2])
            def _():
                forward(1 + side[0], slot).wait_recv()

    lax.fori_loop(0, count + -(-LAST_LAG // PARTS), step, 0)

    if shift:

        @when(core == 0)
        def _():
            for extra in range(shift):
                give_back(extra).wait_recv()
                out_ref[0, :, :, lanes_of(heads - shift + extra)] = back_recv[extra]
                for copy in give(extra):
                    copy.wait_send()

        @when(core == 1)
        def _():
            for extra in range(shift):
                give_back(extra).wait_send()

    @when(prev1)
    def _():
        send_qb(0).wait_send()

        @when(has1)
        def _():
            send_qb(1).wait_send()

    @when(has2)
    def _():
        for slot in range(EARLY):
            forward(0, slot).wait_send()
            for side in sides:

                @when(side[2])
                def _():
                    forward(1 + side[0], slot).wait_send()

    @each_slot
    def _(slot):
        for side in sides:

            @when(side[2])
            def _():
                send_kv(side, slot).wait_send()

        for part in range(PARTS):

            @when(prev1)
            def _():
                send_q(0, slot, part).wait_send()

            @when(prev1, has1, slot >= EARLY)
            def _():
                send_q(1, slot, part).wait_send()

            @when(has1)
            def _():
                for copy in send_o(1, slot, part):
                    copy.wait_send()

            @when(has2, slot >= EARLY)
            def _():
                for copy in send_o(2, slot, part):
                    copy.wait_send()


def solution(mesh):
    frames, rows = mesh.shape["tm"], mesh.shape["space"]
    shift = SHIFT if mesh.shape["head"] == 2 else 0

    def on_device(queries, keys, values, window):
        _, _, columns, channels = queries.shape
        slots = channels // HDIM + shift
        tokens = TILE * columns
        span = tokens // PARTS
        beside = min(rows - 1, 2)
        block = (TILE, columns, HDIM)
        spare = max(shift, 1)
        dma = pltpu.SemaphoreType.DMA
        operands = [
            pltpu.with_memory_space_constraint(a, pltpu.HBM)
            for a in (queries, keys, values, window)
        ]
        return pl.pallas_call(
            functools.partial(kernel, frames, rows, shift),
            out_shape=jax.ShapeDtypeStruct(queries.shape, jnp.bfloat16),
            in_specs=[pl.BlockSpec(memory_space=pl.ANY)] * 4,
            out_specs=pl.BlockSpec(memory_space=pltpu.VMEM),
            scratch_shapes=[
                pltpu.VMEM((3, slots, PARTS, TILE, columns // PARTS, HDIM), jnp.bfloat16),
                pltpu.VMEM((1 + beside, slots, 2, *block), jnp.bfloat16),
                pltpu.VMEM((1 + beside, max(EARLY, 1), 2, *block), jnp.bfloat16),
                pltpu.VMEM((3, PARTS, columns // PARTS, HDIM), jnp.bfloat16),
                pltpu.VMEM((3, (1 + beside) * tokens, HDIM), jnp.bfloat16),
                pltpu.VMEM((2, slots, PARTS, HDIM, span), jnp.bfloat16),
                pltpu.VMEM((2, slots, PARTS, HDIM, span), jnp.bfloat16),
                pltpu.VMEM((2, slots, PARTS, 1, span), jnp.float32),
                pltpu.VMEM((2, slots, PARTS, 1, span), jnp.float32),
                pltpu.VMEM((2, slots, PARTS, HDIM, span), jnp.float32),
                pltpu.VMEM((2, slots, PARTS, 1, span), jnp.float32),
                pltpu.VMEM((spare, *block), jnp.bfloat16),
                pltpu.VMEM((spare, *block), jnp.bfloat16),
                pltpu.SMEM(window.shape, jnp.int32),
                pltpu.SemaphoreType.REGULAR,
                dma((slots, 2 + PARTS)),
                dma,
                dma((max(beside, 1), slots)),
                dma((max(beside, 1), slots)),
                dma((1 + beside, max(EARLY, 1))),
                dma((1 + beside, max(EARLY, 1))),
                dma((2, slots, PARTS)),
                dma((2, slots, PARTS)),
                dma((2,)),
                dma((2,)),
                dma((2, slots, PARTS, 2)),
                dma((2, slots, PARTS, 2)),
                dma((spare, 2 + PARTS)),
                dma((spare, 2 + PARTS)),
                dma((spare,)),
                dma((spare,)),
            ],
            compiler_params=pltpu.CompilerParams(
                collective_id=0, has_side_effects=True, vmem_limit_bytes=VMEM_LIMIT
            ),
        )(*operands)

    placed = P(("group", "tm"), "space", None, "head")
    return jax.shard_map(
        on_device,
        mesh=mesh,
        in_specs=(placed, placed, placed, P(("group", "tm"), "space", None, None)),
        out_specs=placed,
        check_vma=False,
    )
```

time: 51.5 us -> 49.1 us (0.953)
  Pallas kernels: 50.2 us -> 48 us
    pallas_call x1, Pallas kernels: 50.2 us -> 48 us  [on_device(): pl.pallas_call(functools.partial(kernel, frames, rows, shift), out_shape=...]
where the time goes in v2:
time: 49.1 us; the launch traced here: 48.9 us
  Pallas kernels  48 us (98%)
  local copies, waits for them, and re-layouts  0.88 us (2%)
    pallas_call x1, Pallas kernels, on_device(): pl.pallas_call(functools.partial(kernel, frames, rows, shift), out_shape=...  48 us

profile of v2, /device:TPU:24, one launch (start us, length us, event | category | flops | bytes accessed | tf_op | source)
XLA Modules:
  0.0 48.9 jit_solution(15188466323072106919)
XLA Ops:
  0.0 48.0 %shard_map.46 = bf16[1,8,32,1536]{3,2,1,0:T(8,128)(2,1)S(1)} custom-call(bf16[1,8,32,1536]{3,2,1,0:T(8,128)(2,1)} %q_hbm.1, bf16[1,8,32,1536]{3,2,1,0:T(8,128)(2,1)} %k_hbm.1, bf16[1,8,32,1536]{3,2,1,0:T(8,128)(2,1)} %v_hbm.1, s32[1,1,4,27]{3,2,1,0:T(4,128)} %win_hbm.1), custom_call_target="tpu_custom_call" | custom-call | tf_op jit(solution)/shard_map/pallas_call | solution.py:668
  48.1 0.9 %copy.6 = bf16[1,8,32,1536]{3,2,1,0:T(8,128)(2,1)} copy(bf16[1,8,32,1536]{3,2,1,0:T(8,128)(2,1)S(1)} %shard_map.46) | data formatting | bytes 1572864

commit v3 on v2

--- a/solution.py
+++ b/solution.py
@@ -15,7 +15,7 @@
 SHIFT = 0
 DIRECT = 0
 OWN_LAG, RELAY_LAG, KV_LAG, FAR_LAG, NEAR_LAG = -3, -1, 1, 1, 1
-MERGE_LAG, EARLY_LAG, HOME_LAG, LAST_LAG = 2, 1, 1, 5
+MERGE_LAG, EARLY_LAG, HOME_LAG, LAST_LAG = 2, 1, 1, 4
 FORWARD_AT = 0
 MASKED = -float(2**17)
 EXP2_SCALE = HDIM ** (-0.5) * math.log2(math.e)
@@ -189,7 +189,7 @@
         )
 
     def send_o(dt, slot, part, hops=1):
-        pairs = ((o_send, o_recv), (lse_send, lse_recv))
+        pairs = ((lse_send, lse_recv), (o_send, o_recv))
         return [
             remote(
                 src.at[dt - 1, slot, part],

time: 49.1 us -> 49 us (level)
  no operation moved by 1% of the time
where the time goes in v3:
time: 49 us; the launch traced here: 48.9 us
  Pallas kernels  48 us (98%)
  local copies, waits for them, and re-layouts  0.88 us (2%)
    pallas_call x1, Pallas kernels, on_device(): pl.pallas_call(functools.partial(kernel, frames, rows, shift), out_shape=...  48 us

profile of v3, /device:TPU:24, one launch (start us, length us, event | category | flops | bytes accessed | tf_op | source)
XLA Modules:
  0.0 48.9 jit_solution(13666049767138304027)
XLA Ops:
  0.0 48.0 %shard_map.46 = bf16[1,8,32,1536]{3,2,1,0:T(8,128)(2,1)S(1)} custom-call(bf16[1,8,32,1536]{3,2,1,0:T(8,128)(2,1)} %q_hbm.1, bf16[1,8,32,1536]{3,2,1,0:T(8,128)(2,1)} %k_hbm.1, bf16[1,8,32,1536]{3,2,1,0:T(8,128)(2,1)} %v_hbm.1, s32[1,1,4,27]{3,2,1,0:T(4,128)} %win_hbm.1), custom_call_target="tpu_custom_call" | custom-call | tf_op jit(solution)/shard_map/pallas_call | solution.py:668
  48.0 0.9 %copy.6 = bf16[1,8,32,1536]{3,2,1,0:T(8,128)(2,1)} copy(bf16[1,8,32,1536]{3,2,1,0:T(8,128)(2,1)S(1)} %shard_map.46) | data formatting | bytes 1572864
